TPU v7x, 256 devices: a whole 4x4x8 slice. The times are simulated.
256 devices in a mesh: dp: 32 (over y, z), group: 8 (over x, core).
Axes of the slice: x: 4, y: 4, z: 8, core: 2. Of those that a mesh axis runs over, the one named last changes fastest.
Arguments:
- keys: int32 [131072], P(('dp', 'group')), may hold values from 0 to 1073741823
- cut: int32 [1], replicated, may hold values from 256 to 1023
- owner: int32 [131072, 1], P(('dp', 'group')), may hold values from 0 to 31; in each aligned block of 512 rows (0 to 511, 512 to 1023, ...) at most 32 rows name the same one
- tokens: int32 [131072, 2048], P(('dp', 'group')), may hold values from 0 to 128255
Outputs:
- histogram: int32 [4096], replicated
- packed_rows: int32 [262144, 2048], P(('dp', 'group'))
- packed_weights: float32 [262144], P(('dp', 'group'))
Inputs may be any that keep to these rules, and one draw needn't show every extreme that they name: Among the examples of one device, at most 32 have the same owner, and some owner has exactly 32.
All inputs are finite; a program needn't handle non-finite values.
Results may differ from a plain program's by a relative error of at most 0.0003.
Values sent between devices are 32-bit elements; how exact they have to be, the bound alone decides.
A program may use at most 128 MiB of HBM per device.

v0:
```python
import jax
import jax.numpy as jnp
from jax import lax
from jax.sharding import Mesh
from jax.sharding import PartitionSpec as P

BINS = 4096
BIN_WIDTH = 262144
DP = ("dp_0", "dp_1")
GROUP = ("group_0", "group_1")
DP_GROUP = ("dp_0", "dp_1", "group_0", "group_1")


def neutral_like(value, identity):
    return jnp.broadcast_to(jnp.asarray(identity, value.dtype), value.shape)


def prefix_by_axis(value, axes, combine, identity):
    before = start = neutral_like(value, identity)
    so_far = value
    for axis in reversed(axes):
        count, index = (lax.axis_size(axis), lax.axis_index(axis))
        pieces = lax.all_gather(so_far, axis)
        inside, so_far = (start, start)
        for k in range(count):
            passed = k < index
            so_far = combine(so_far, pieces[k])
            inside = jnp.where(passed, so_far, inside)
        before = combine(inside, before)
    return before


def split_up(value, dim, count):
    before, after = (value.shape[:dim], value.shape[dim + 1 :])
    return jnp.moveaxis(value.reshape(*before, count, -1, *after), dim, 0)


def laid_out(tiles, dim):
    tiles = jnp.moveaxis(tiles, 0, dim)
    dims = tiles.shape
    return tiles.reshape(*dims[:dim], dims[dim] * dims[dim + 1], *dims[dim + 2 :])


def exchange_both(value, axis, axes, splits, concats):
    sizes = [lax.axis_size(a) for a in axes]
    tiles = split_up(value, splits[0], sizes[0])
    tiles = jnp.moveaxis(split_up(tiles, splits[1] + 1, sizes[1]), 0, 1)
    inside = tiles.shape[2:]
    tiles = tiles.reshape(-1, *inside)
    tiles = lax.all_to_all(tiles, axis, split_axis=0, concat_axis=0, tiled=True)
    tiles = laid_out(tiles.reshape(*sizes, *inside), concats[0] + 1)
    return laid_out(tiles, concats[1])


def add_counts(earlier, later):
    return earlier + later


def body(keys, cut, owner, tokens):
    examples = keys.shape[0]
    width = tokens.shape[1]
    n_owner = lax.axis_size(DP)
    n_member = lax.axis_size(GROUP)
    slots = 2 * examples // (n_owner * n_member)
    capacity = 2 * examples
    bins_of = keys // BIN_WIDTH
    local_hist = jnp.zeros((BINS,), jnp.float32).at[bins_of].add(1.0)
    kept = bins_of >= cut[0]
    dest = owner[:, 0]
    onehot = (
        (dest[:, None] == jnp.arange(n_owner, dtype=jnp.int32)[None, :]) & kept[:, None]
    ).astype(jnp.int32)
    counts = jnp.sum(onehot, axis=0).astype(jnp.float32)
    before = prefix_by_axis(counts, DP_GROUP, add_counts, jnp.zeros_like(counts))
    hist = lax.psum(local_hist, DP_GROUP)
    running = jnp.cumsum(onehot, axis=0) - onehot
    local_rank = jnp.sum(running * onehot, axis=1)
    offset = jnp.sum(before.astype(jnp.int32)[None, :] * onehot, axis=1)
    rank = offset + local_rank
    member = rank % n_member
    outside = n_owner * n_member * slots
    position_send = jnp.where(
        kept, (dest * n_member + member) * slots + local_rank // n_member, outside
    )
    send_rows = jnp.zeros((outside, width), jnp.int32).at[position_send].set(tokens, mode="drop")
    details = jnp.stack([rank // n_member, keys], axis=1)
    send_meta = jnp.full((outside, 2), -1, jnp.int32).at[position_send].set(details, mode="drop")
    send_rows = send_rows.reshape(n_owner, n_member, slots, width)
    send_meta = send_meta.reshape(n_owner, n_member, slots, 2)
    got_rows, got_meta = (
        exchange_both(send_rows, DP_GROUP, (DP, GROUP), (0, 1), (0, 1)),
        exchange_both(send_meta, DP_GROUP, (DP, GROUP), (0, 1), (0, 1)),
    )
    got_rows = got_rows.reshape(-1, width)
    got_meta = got_meta.reshape(-1, 2)
    slot = got_meta[:, 0]
    valid = slot >= 0
    target = jnp.where(valid, slot, capacity)
    suffix = jnp.cumsum(hist[::-1])[::-1]
    total = jnp.maximum(suffix[cut[0]], 1.0)
    got_bins = jnp.clip(got_meta[:, 1] // BIN_WIDTH, 0, BINS - 1)
    weight = jnp.where(valid, suffix[got_bins] / total, 0.0)
    packed_rows = jnp.zeros((capacity, width), jnp.int32).at[target].set(got_rows, mode="drop")
    packed_weights = jnp.zeros((capacity,), jnp.float32).at[target].set(weight, mode="drop")
    return (hist.astype(jnp.int32), packed_rows, packed_weights)


def solution(mesh):
    torus = Mesh(mesh.devices.reshape(4, 8, 4, 2), ("dp_0", "dp_1", "group_0", "group_1"))
    placed = (P(DP_GROUP), P(), P(DP_GROUP, None), P(DP_GROUP, None))
    return jax.shard_map(
        body,
        mesh=torus,
        in_specs=placed,
        out_specs=(P(), P(DP_GROUP, None), P(DP_GROUP)),
        check_vma=False,
    )
```

profile of v0, /device:TPU:1, one launch (start us, length us, event | category | flops | bytes accessed | tf_op | source)
XLA Modules:
  0.0 360.7 jit_solution(18366167405808590215)
XLA Ops:
  1.3 0.7 broadcast_compare_fusion
  2.0 0.8 convert_reduce_fusion
  2.8 1.3 dynamic-slice
  4.8 5.3 %all-reduce = f32[64]{0:T(128)S(1)} all-reduce(f32[64]{0:T(128)S(1)} %convert_dynamic-update-slice_fusion), channel_id=2, replica_groups=mesh['dp_0'=4,'dp_1'=8,'group_0'=4,'group_1'=2] {'group_1'}, use_global_device_ids=true, to_apply=%add | all-reduce | flops 64 | bytes 512
  10.1 1.3 dynamic-slice.1
  12.2 6.7 %all-reduce.1 = f32[128]{0:T(128)S(1)} all-reduce(f32[128]{0:T(128)S(1)} %fusion.35), channel_id=3, replica_groups=mesh['dp_0'=4,'dp_1'=8,'group_0'=4,'group_1'=2] {'group_0'}, use_global_device_ids=true, to_apply=%add.1 | all-reduce | flops 128 | bytes 1024
  19.0 15.4 %all-gather.2 = f32[8,1,32]{2,1,0:T(1,128)S(1)} all-gather(f32[1,1,32]{2,1,0:T(1,128)S(1)} %fusion.37), channel_id=1, replica_groups=mesh['dp_0'=4,'dp_1'=8,'group_0'=4,'group_1'=2] {'dp_1'}, dimensions={0}, use_global_device_ids=true | all-gather | bytes 1152 | tf_op jit(solution)/shard_map/all_gather | solution.py:23
  34.4 7.9 %all-gather.3 = f32[4,1,32]{2,1,0:T(1,128)S(1)} all-gather(f32[1,1,32]{2,1,0:T(1,128)S(1)} %bitcast.115), channel_id=1, replica_groups=mesh['dp_0'=4,'dp_1'=8,'group_0'=4,'group_1'=2] {'dp_0'}, dimensions={0}, use_global_device_ids=true | all-gather | bytes 640 | tf_op jit(solution)/shard_map/all_gather | solution.py:23
  43.1 1.2 reduce-window.15
  44.6 0.8 select_reduce_fusion
  45.4 0.7 compare_select_fusion.6
  46.1 0.7 pad_add_fusion
  47.0 1.8 scatter_custom_fusion.1
  48.8 2.3 copy.14
  51.1 13.2 %all-to-all-start = ((s32[256,1,1,4,2]{3,4,2,1,0:T(2,128)}), s32[256,1,1,4,2]{3,4,2,1,0:T(2,128)S(1)}, u32[]{:S(2)}, u32[]{:S(2)}) async-start(s32[256,1,1,4,2]{3,4,2,1,0:T(2,128)} %copy.14), calls=%async_computation | async-start | bytes 524288 | tf_op jit(solution)/shard_map/all_to_all | solution.py:50
  64.3 8.6 %scatter_custom_fusion.2 = s32[1024,2048]{1,0:T(8,128)} fusion(s32[512]{0:T(512)S(1)} %get-tuple-element.5, s32[512,2048]{1,0:T(8,128)} %param.7, s32[]{:T(128)} %constant.97.clone.1), kind=kCustom, calls=%fused_computation.8 | custom fusion | bytes 8389120 | tf_op jit(solution)/shard_map/scatter | solution.py:85
  72.9 9.8 %reshape_transpose_transpose_reshape_reshape_reshape.7 = s32[256,1,1,4,2048]{4,3,0,2,1:T(4,128)} reshape(s32[1024,2048]{1,0:T(8,128)} %scatter_custom_fusion.2) | data formatting | bytes 16777216 | tf_op jit(solution)/shard_map/reshape;transpose;transpose;reshape;reshape;reshape | solution.py:49
  82.7 14.9 %all-to-all-start.1 = ((s32[256,1,1,4,2048]{4,3,2,1,0:T(4,128)}), s32[256,1,1,4,2048]{4,3,2,1,0:T(4,128)}, u32[]{:S(2)}, u32[]{:S(2)}) async-start(s32[256,1,1,4,2048]{4,3,2,1,0:T(4,128)} %bitcast.102), calls=%async_computation.1 | async-start | bytes 16777216 | tf_op jit(solution)/shard_map/all_to_all | solution.py:50
  97.6 3.3 scatter_custom_fusion
  100.8 222.9 %psum.7 = f32[4096]{0:T(1024)S(1)} all-reduce(f32[4096]{0:T(1024)S(1)} %scatter_custom_fusion), channel_id=1, replica_groups=mesh['dp_0'=4,'dp_1'=8,'group_0'=4,'group_1'=2] {'dp_0','dp_1','group_0'..., use_global_device_ids=true, to_apply=%region_1.2 | all-reduce | flops 4096 | bytes 32768 | tf_op jit(solution)/shard_map/psum | solution.py:75
  326.6 6.2 %gather_fusion = f32[1024]{0:T(1024)S(1)} fusion(f32[4096]{0:T(1024)S(1)} %rev.7, s32[1024]{0:T(1024)S(1)} %broadcast_clamp_fusion), kind=kCustom, calls=%fused_computation | custom fusion | bytes 12288 | tf_op jit(solution)/shard_map/gather | solution.py:102
  332.8 4.9 %scatter_custom_fusion.4 = f32[1024]{0:T(1024)} fusion(s32[1024]{0:T(1024)S(1)} %bitcast.116, f32[1024]{0:T(1024)S(1)} %divide_select_fusion, f32[]{:T(128)} %constant.95.clone.1), kind=kCustom, calls=%fused_computation.65 | custom fusion | bytes 4100 | tf_op jit(solution)/shard_map/scatter | solution.py:104
  337.7 10.0 %reshape.165 = s32[1024,2048]{1,0:T(8,128)} reshape(s32[32,8,1,4,2048]{4,3,1,0,2:T(4,128)} %bitcast.31) | data formatting | bytes 16777216 | tf_op jit(solution)/shard_map/reshape;reshape | solution.py:94
  347.7 13.0 %scatter_custom_fusion.3 = s32[1024,2048]{1,0:T(8,128)} fusion(s32[1024]{0:T(1024)S(1)} %bitcast.117, s32[1024,2048]{1,0:T(8,128)} %reshape.165, s32[]{:T(128)} %constant.97.clone.1), kind=kCustom, calls=%fused_computation.6 | custom fusion | bytes 8389120 | tf_op jit(solution)/shard_map/scatter | solution.py:103
  (32 shorter events, 3.8 us)
Async XLA Ops:
  51.1 31.6 %all-to-all-start = ((s32[256,1,1,4,2]{3,4,2,1,0:T(2,128)}), s32[256,1,1,4,2]{3,4,2,1,0:T(2,128)S(1)}, u32[]{:S(2)}, u32[]{:S(2)}) async-start(s32[256,1,1,4,2]{3,4,2,1,0:T(2,128)} %copy.14), calls=%async_computation | async-start | bytes 524288 | tf_op jit(solution)/shard_map/all_to_all | solution.py:50
  82.7 255.0 %all-to-all-start.1 = ((s32[256,1,1,4,2048]{4,3,2,1,0:T(4,128)}), s32[256,1,1,4,2048]{4,3,2,1,0:T(4,128)}, u32[]{:S(2)}, u32[]{:S(2)}) async-start(s32[256,1,1,4,2048]{4,3,2,1,0:T(4,128)} %bitcast.102), calls=%async_computation.1 | async-start | bytes 16777216 | tf_op jit(solution)/shard_map/all_to_all | solution.py:50
where the time goes:
time: 362 us; the launch traced here: 361 us
  blocking collectives  258 us (71%)
  local copies, waits for them, and re-layouts  60.7 us (17%)
  starting transfers between devices  28 us (8%)
  other arithmetic  10.4 us (3%)
    psum x1, blocking collectives, body(): hist = lax.psum(local_hist, DP_GROUP)  223 us
    all_to_all x2, starting transfers between devices, exchange_both(): tiles = lax.all_to_all(tiles, axis, split_axis=0, concat_axis=0, tiled=True)  28 us
    all_gather x2, blocking collectives, prefix_by_axis(): pieces = lax.all_gather(so_far, axis)  23.3 us
    scatter x1, local copies, waits for them, and re-layouts, body(): jnp.zeros((capacity, width), jnp.int32).at[target]  13 us
    another operation x2, local copies, waits for them, and re-layouts, exchange_both(): tiles = tiles.reshape(-1, *inside)  12.1 us
    unnamed x2, blocking collectives  12 us
    another operation x1, local copies, waits for them, and re-layouts, body(): got_rows = got_rows.reshape(-1, width)  10 us
    scatter x1, local copies, waits for them, and re-layouts, body(): jnp.zeros((outside, width), jnp.int32).at[position_send]  8.6 us
  transfers between devices with their start and end apart: 2, of which 0 were waited for; matrix products, arithmetic and copies ran while one was open for 10% of the time, Pallas kernels for 0%

commit v1 on v0

v1 whole, which is shorter than its diff:
```python
import functools

import jax
import jax.numpy as jnp
from jax import lax
from jax.experimental import pallas as pl
from jax.experimental.pallas import tpu as pltpu
from jax.sharding import Mesh
from jax.sharding import PartitionSpec as P

BINS = 4096
BIN_WIDTH = 262144
NY, NZ, NX, NC = 4, 8, 4, 2
NO = NY * NZ
NM = NX * NC
NS = NO * NM
PLANE = NY * NM
EX = 512
RECV = 1024
MESH_ID = pl.DeviceIdType.MESH
AXES = ("y", "z", "x", "c")

TIERS = (
    (208, 168, 120, 72),
    (232, 192, 136, 80),
    (256, 208, 152, 96),
    (384, 264, 256, 128),
)
PLUS, OWN, MINUS = 0, 384, 512
PACKED = 896


def me():
    return tuple(lax.axis_index(a) for a in AXES)


def signal_peers(bar, z, y, x, c):
    def ring(d, _):
        pl.semaphore_signal(bar, 1, device_id={"z": lax.rem(z + d, NZ)}, device_id_type=MESH_ID)
        return 0

    def plane(r, _):
        pl.semaphore_signal(bar, 1, device_id=in_plane(r, y, x, c), device_id_type=MESH_ID)
        return 0

    lax.fori_loop(1, NZ, ring, 0)
    lax.fori_loop(1, PLANE, plane, 0)
    pl.semaphore_wait(bar, NZ - 1 + PLANE - 1)


def in_plane(r, y, x, c):
    return {
        "y": lax.rem(y + r // NM, NY),
        "x": lax.rem(x + (r // NC) % NX, NX),
        "c": lax.rem(c + r % NC, NC),
    }


def counts_kernel(row_ref, out_ref, ring_ref, send1, send2, recv1, recv2):
    y, z, x, c = me()
    signal_peers(pltpu.get_barrier_semaphore(), z, y, x, c)

    def ring_copy(d):
        return pltpu.make_async_remote_copy(
            row_ref.at[0], ring_ref.at[z], send1, recv1,
            device_id={"z": lax.rem(z + d, NZ)}, device_id_type=MESH_ID)

    def start_ring(d, _):
        ring_copy(d).start()
        return 0

    lax.fori_loop(1, NZ, start_ring, 0)
    pltpu.make_async_copy(row_ref.at[0], ring_ref.at[z], recv1).start()
    pltpu.make_async_copy(ring_ref, ring_ref, recv1).wait()
    p = y * NM + x * NC + c

    def start_plane(r, _):
        pltpu.make_async_remote_copy(
            ring_ref, out_ref.at[p], send2, recv2,
            device_id=in_plane(r, y, x, c), device_id_type=MESH_ID).start()
        return 0

    lax.fori_loop(1, PLANE, start_plane, 0)
    out_ref[pl.ds(p, 1)] = ring_ref[...].reshape(1, NZ, 1, 128)
    pltpu.make_async_copy(out_ref.at[pl.ds(0, PLANE - 1)], out_ref.at[pl.ds(0, PLANE - 1)], recv2).wait()
    pltpu.make_async_copy(ring_ref.at[pl.ds(0, NZ - 1)], ring_ref.at[pl.ds(0, NZ - 1)], send1).wait()
    pltpu.make_async_copy(out_ref.at[pl.ds(0, PLANE - 1)], out_ref.at[pl.ds(0, PLANE - 1)], send2).wait()


def exchange_counts(row):
    return pl.pallas_call(
        counts_kernel,
        out_shape=jax.ShapeDtypeStruct((PLANE, NZ, 1, 128), jnp.int32),
        in_specs=[pl.BlockSpec(memory_space=pltpu.VMEM)],
        out_specs=pl.BlockSpec(memory_space=pltpu.VMEM),
        scratch_shapes=[
            pltpu.VMEM((NZ, 1, 128), jnp.int32),
            pltpu.SemaphoreType.DMA, pltpu.SemaphoreType.DMA, pltpu.SemaphoreType.DMA, pltpu.SemaphoreType.DMA,
        ],
        compiler_params=pltpu.CompilerParams(collective_id=0, has_side_effects=True),
        name="exchange_counts",
    )(row)


def pack_kernel(pos_ref, tok_ref, out_ref):
    def row(e, _):
        p = pos_ref[e]

        @pl.when(p >= 0)
        def _():
            start = (e // 8) * 128 + e % 8
            out_ref[pl.ds(pl.multiple_of(p * 16, 16), 16), :] = tok_ref[pl.ds(start, 16, stride=8), :]

        return 0

    lax.fori_loop(0, EX, row, 0, unroll=4)


def pack_rows(pos, tok):
    return pl.pallas_call(
        pack_kernel,
        out_shape=jax.ShapeDtypeStruct((PACKED * 16, 128), jnp.int32),
        in_specs=[pl.BlockSpec(memory_space=pltpu.SMEM), pl.BlockSpec(memory_space=pltpu.VMEM)],
        out_specs=pl.BlockSpec(memory_space=pltpu.VMEM),
        name="pack_rows",
    )(pos, tok)


def main_kernel(caps, idx_ref, pk_ref, bin_ref, hist_ref,
                rows_out, hist_out, bins_out,
                p1, m1, p2, m2, p3, m3, far, stage, hz, hp, bz,
                zsend, zrecv, psend, precv, hzsend, hzrecv, hpsend, hprecv, bzsend, bzrecv, bpsend, bprecv):
    y, z, x, c = me()
    signal_peers(pltpu.get_barrier_semaphore(), z, y, x, c)
    c1, c2, c3, c4 = caps
    up, down = lax.rem(z + 1, NZ), lax.rem(z + NZ - 1, NZ)
    plane = y * NM + x * NC + c

    def hop(src, dst, lo, hi, at_src, at_dst, sem, to):
        copy = pltpu.make_async_remote_copy(
            src.at[pl.ds(at_src + lo, hi - lo)],
            dst.at[pl.ds(at_dst + lo, hi - lo)],
            zsend.at[sem], zrecv.at[sem], device_id={"z": to}, device_id_type=MESH_ID)
        copy.start()
        return copy

    h1 = [hop(pk_ref, p1, 0, c2, PLUS, 0, 0, up), hop(pk_ref, m1, 0, c2, MINUS, 0, 1, down),
          hop(pk_ref, p1, c2, c1, PLUS, 0, 2, up), hop(pk_ref, m1, c2, c1, MINUS, 0, 3, down)]

    def ring_small(d, _):
        to = {"z": lax.rem(z + d, NZ)}
        pltpu.make_async_remote_copy(hist_ref, hz.at[z], hzsend, hzrecv, device_id=to, device_id_type=MESH_ID).start()
        pltpu.make_async_remote_copy(bin_ref, bz.at[z], bzsend, bzrecv, device_id=to, device_id_type=MESH_ID).start()
        return 0

    lax.fori_loop(1, NZ, ring_small, 0)
    hz[pl.ds(z, 1)] = hist_ref[...].reshape(1, 32, 128)
    bz[pl.ds(z, 1)] = bin_ref[...].reshape(1, 4, 128)

    def send_chunk(delta, src):
        base = delta * PLANE * 4

        def gather(i, _):
            stage[base + i] = src[idx_ref[base + i]]
            return 0

        lax.fori_loop(0, PLANE * 4, gather, 0, unroll=8)
        zs = lax.rem(z + NZ - delta, NZ)
        s = ((y * NZ + zs) * NX + x) * NC + c

        def send(r, _):
            pltpu.make_async_remote_copy(
                stage.at[pl.ds((delta * PLANE + r) * 4, 4)],
                rows_out.at[pl.ds(s * 4, 4)],
                psend, precv, device_id=in_plane(r, y, x, c), device_id_type=MESH_ID).start()
            return 0

        lax.fori_loop(1, PLANE, send, 0)
        pltpu.make_async_copy(stage.at[pl.ds(delta * PLANE * 4, 4)], rows_out.at[pl.ds(s * 4, 4)], precv).start()

    send_chunk(0, pk_ref)

    seven = hz.at[pl.ds(0, NZ - 1)]
    pltpu.make_async_copy(seven, seven, hzrecv).wait()
    seven_b = bz.at[pl.ds(0, NZ - 1)]
    pltpu.make_async_copy(seven_b, seven_b, bzrecv).wait()
    total = hz[0]
    for k in range(1, NZ):
        total = total + hz[k]
    hp[pl.ds(plane, 1)] = total.reshape(1, 32, 128)
    bins_out[pl.ds(plane, 1)] = bz[...].reshape(1, NZ, 4, 128)

    def plane_small(r, _):
        to = in_plane(r, y, x, c)
        pltpu.make_async_remote_copy(hp.at[plane], hp.at[plane], hpsend, hprecv, device_id=to, device_id_type=MESH_ID).start()
        pltpu.make_async_remote_copy(bz, bins_out.at[plane], bpsend, bprecv, device_id=to, device_id_type=MESH_ID).start()
        return 0

    lax.fori_loop(1, PLANE, plane_small, 0)
    others = hp.at[pl.ds(0, PLANE - 1)]
    pltpu.make_async_copy(others, others, hprecv).wait()
    others_b = bins_out.at[pl.ds(0, PLANE - 1)]
    pltpu.make_async_copy(others_b, others_b, bprecv).wait()
    total = hp[0]
    for k in range(1, PLANE):
        total = total + hp[k]
    hist_out[...] = total

    h1[0].wait_recv()
    h2 = [hop(p1, p2, 0, c3, 0, 0, 4, up)]
    h1[1].wait_recv()
    h2 += [hop(m1, m2, 0, c3, 0, 0, 5, down), hop(p1, p2, c3, c2, 0, 0, 6, up), hop(m1, m2, c3, c2, 0, 0, 7, down)]
    h1[2].wait_recv()
    send_chunk(1, p1)
    h1[3].wait_recv()
    send_chunk(7, m1)
    h2[0].wait_recv()
    h3 = [hop(p2, p3, 0, c4, 0, 0, 8, up)]
    h2[1].wait_recv()
    h3 += [hop(m2, m3, 0, c4, 0, 0, 9, down), hop(p2, p3, c4, c3, 0, 0, 10, up), hop(m2, m3, c4, c3, 0, 0, 11, down)]
    h2[2].wait_recv()
    send_chunk(2, p2)
    h2[3].wait_recv()
    send_chunk(6, m2)
    h3[0].wait_recv()
    h4 = [hop(p3, far, 0, c4, 0, 0, 12, up)]
    h3[1].wait_recv()
    h4 += [hop(m3, far, 0, c4, 0, 128, 13, down)]
    h3[2].wait_recv()
    send_chunk(3, p3)
    h3[3].wait_recv()
    send_chunk(5, m3)
    h4[0].wait_recv()
    h4[1].wait_recv()
    send_chunk(4, far)

    for copy in h1 + h2 + h3 + h4:
        copy.wait_send()
    pltpu.make_async_copy(seven, seven, hzsend).wait()
    pltpu.make_async_copy(seven_b, seven_b, bzsend).wait()
    pltpu.make_async_copy(others, others, hpsend).wait()
    pltpu.make_async_copy(others_b, others_b, bpsend).wait()
    sent = stage.at[pl.ds(0, NZ * (PLANE - 1) * 4)]
    pltpu.make_async_copy(sent, sent, psend).wait()
    pltpu.make_async_copy(stage, rows_out, precv).wait()


def exchange_rows(tier, idx, packed, bins, hist):
    caps = TIERS[tier]
    c1, c2, c3, c4 = caps
    vmem = pl.BlockSpec(memory_space=pltpu.VMEM)
    rows = lambda n: pltpu.VMEM((n, 16, 128), jnp.int32)
    dma = pltpu.SemaphoreType.DMA
    return pl.pallas_call(
        functools.partial(main_kernel, caps),
        out_shape=(
            jax.ShapeDtypeStruct((NS * 4, 16, 128), jnp.int32),
            jax.ShapeDtypeStruct((32, 128), jnp.float32),
            jax.ShapeDtypeStruct((PLANE, NZ, 4, 128), jnp.float32),
        ),
        in_specs=[pl.BlockSpec(memory_space=pltpu.SMEM), vmem, vmem, vmem],
        out_specs=(pl.BlockSpec(memory_space=pl.ANY), vmem, vmem),
        scratch_shapes=[
            rows(c1), rows(c1), rows(c2), rows(c2), rows(c3), rows(c3), rows(256),
            rows(NS * 4),
            pltpu.VMEM((NZ, 32, 128), jnp.float32), pltpu.VMEM((PLANE, 32, 128), jnp.float32),
            pltpu.VMEM((NZ, 4, 128), jnp.float32),
            dma((14,)), dma((14,)), dma, dma, dma, dma, dma, dma, dma, dma, dma, dma,
        ],
        compiler_params=pltpu.CompilerParams(
            collective_id=1 + tier, has_side_effects=True, vmem_limit_bytes=60 * 1024 * 1024),
        name=f"exchange_rows_{tier}",
    )(idx, packed, bins, hist)


def unpack_kernel(idx_ref, rows_ref, out_ref):
    block = out_ref.shape[0] // 16
    first = pl.program_id(0) * block

    def row(t, _):
        k = idx_ref[first + t]
        value = rows_ref[pl.ds(pl.multiple_of(jnp.maximum(k, 0) * 16, 16), 16), :]
        out_ref[pl.ds((t // 8) * 128 + t % 8, 16, stride=8), :] = jnp.where(k >= 0, value, 0)
        return 0

    lax.fori_loop(0, block, row, 0, unroll=8)


def unpack_rows(idx, rows):
    block = 128
    return pl.pallas_call(
        unpack_kernel,
        grid=(RECV // block,),
        out_shape=jax.ShapeDtypeStruct((RECV * 16, 128), jnp.int32),
        in_specs=[pl.BlockSpec(memory_space=pltpu.SMEM), pl.BlockSpec(memory_space=pltpu.VMEM)],
        out_specs=pl.BlockSpec((block * 16, 128), lambda i: (i, 0)),
        name="unpack_rows",
    )(idx, rows)


def layout_of(counts, z):
    owner = jnp.arange(NO)
    delta = (owner % NZ - z[..., None]) % NZ
    yo = owner // NZ
    order = jnp.where(delta <= 4, 4 - delta, delta - 4)
    side = jnp.where(delta == 4, 2, jnp.where(delta == 0, 3, jnp.where(delta < 4, 0, 1)))
    place = order * NY + yo
    before = (place[..., None, :] < place[..., :, None]) & (side[..., None, :] == side[..., :, None])
    inside = jnp.sum(jnp.where(before, counts[..., None, :], 0), axis=-1)
    flow = lambda d: jnp.sum(jnp.where(delta == d, counts, 0), axis=-1)
    f = [flow(d) for d in range(NZ)]
    plus, minus = f[1] + f[2] + f[3], f[5] + f[6] + f[7]
    split = jnp.clip((f[4] + minus - plus) // 2, 0, f[4])
    rest = f[4] - split
    first = inside + jnp.where(side == 0, split[..., None], jnp.where(side == 1, rest[..., None], 0))
    hops = [
        jnp.maximum(plus + split, minus + rest),
        jnp.maximum(f[2] + f[3] + split, f[5] + f[6] + rest),
        jnp.maximum(f[3] + split, f[5] + rest),
        jnp.maximum(split, rest),
    ]
    return first, side, split, hops


def body(keys, cut, owner, tokens):
    y, z, x, c = me()
    group = x * NC + c
    mine = y * NZ + z
    owners = jnp.arange(NO, dtype=jnp.int32)

    bins_of = keys // BIN_WIDTH
    kept = bins_of >= cut[0]
    dest = jnp.where(kept, owner[:, 0], NO)
    e = jnp.arange(EX)
    same = (dest[:, None] == dest[None, :]) & (e[None, :] < e[:, None])
    local_rank = jnp.sum(same.astype(jnp.int32), axis=1)
    onehot = dest[:, None] == owners[None, :]
    counts = jnp.sum(onehot.astype(jnp.int32), axis=0)
    row = jnp.zeros((1, 1, 128), jnp.int32).at[0, 0, :NO].set(counts)
    table = exchange_counts(row)

    first, side, split, _ = layout_of(counts, z)
    pick = lambda v: jnp.sum(jnp.where(onehot, v[None, :], 0), axis=1)
    at, on = pick(first) + local_rank, pick(side)
    far_at = jnp.where(at < split, PLUS + at, MINUS + at - split)
    pos = jnp.where(on == 0, PLUS + at, jnp.where(on == 1, MINUS + at, jnp.where(on == 2, far_at, OWN + at)))
    pos = jnp.where(kept, pos, -1).astype(jnp.int32)
    tiles = tokens.reshape(EX // 8, 8, 16, 128).transpose(0, 2, 1, 3).reshape(EX * 16, 128)
    packed = pack_rows(pos, tiles)

    tri = owners[:, None] < owners[None, :]
    sort_first = jnp.sum(jnp.where(tri, counts[:, None], 0), axis=0)
    sort_pos = jnp.where(kept, pick(sort_first) + local_rank, -1)
    bins_sorted = jnp.sum(jnp.where(sort_pos[None, :] == e[:, None], bins_of[None, :], 0), axis=1)
    bins_sorted = bins_sorted.astype(jnp.float32).reshape(4, 128)
    hi = (bins_of[:, None] // 128 == jnp.arange(32)[None, :]).astype(jnp.bfloat16)
    lo = (bins_of[:, None] % 128 == jnp.arange(128)[None, :]).astype(jnp.bfloat16)
    local_hist = lax.dot_general(hi, lo, (((0,), (0,)), ((), ())), preferred_element_type=jnp.float32)

    table = table.reshape(NY, NM, NZ, 128)[..., :NO]
    by_source = table.transpose(0, 2, 1, 3).reshape(NS, NO)
    s = jnp.arange(NS)
    lower = (s[None, :] < s[:, None]).astype(jnp.float32)
    offset = jnp.dot(lower, by_source.astype(jnp.float32), precision=lax.Precision.HIGHEST).astype(jnp.int32)

    zs_all = (s // NM) % NZ
    _, _, _, hops = layout_of(by_source, zs_all)
    tops = [jnp.max(h) for h in hops]
    tier = jnp.int32(0)
    for caps in TIERS[:-1]:
        fits = functools.reduce(jnp.logical_and, [t <= cap for t, cap in zip(tops, caps)])
        tier = tier + jnp.logical_not(fits).astype(jnp.int32)

    delta = jnp.arange(NZ)
    zs = (z - delta) % NZ
    src = (y * NZ + zs) * NM + group
    k_src, o_src = by_source[src], offset[src]
    first8, side8, split8, _ = layout_of(k_src, zs)
    rel = jnp.arange(PLANE)
    to_owner = ((y + rel // NM) % NY) * NZ + z
    to_member = ((x + (rel // NC) % NX) % NX) * NC + (c + rel % NC) % NC
    take = lambda v: v[:, to_owner][:, :, None]
    lr = (to_member[None, :, None] - take(o_src)) % NM + NM * jnp.arange(4)[None, None, :]
    q = take(first8) + lr
    far_q = jnp.where(q < split8[:, None, None], q, 128 + q - split8[:, None, None])
    q = jnp.where(take(side8) == 2, far_q, q)
    q = q + jnp.where(delta == 0, OWN, 0)[:, None, None]
    idx = jnp.where(lr < take(k_src), q, 0).astype(jnp.int32).reshape(NS * 4)

    branches = [functools.partial(exchange_rows, t) for t in range(len(TIERS))]
    rows, hist, bins_all = lax.switch(tier, branches, idx, packed.reshape(PACKED, 16, 128), bins_sorted, local_hist)
    rows = rows.reshape(NS * 64, 128)

    cnt, off = by_source[:, mine], offset[:, mine]
    lr0 = (group - off) % NM
    n = jnp.maximum(0, (cnt - lr0 + NM - 1) // NM)
    start = jnp.sum(jnp.where(s[None, :] < s[:, None], n[None, :], 0), axis=1)
    slot = jnp.arange(RECV)
    hit = (start[None, :] <= slot[:, None]) & (slot[:, None] < (start + n)[None, :])
    out_idx = jnp.sum(jnp.where(hit, 4 * s[None, :] + slot[:, None] - start[None, :] + 1, 0), axis=1) - 1
    out = unpack_rows(out_idx.astype(jnp.int32), rows)
    packed_rows = out.reshape(RECV // 8, 16, 8, 128).transpose(0, 2, 1, 3).reshape(RECV, 16 * 128)

    hist = hist.reshape(BINS)
    suffix = jnp.cumsum(hist[::-1])[::-1]
    total = jnp.maximum(suffix[cut[0]], 1.0)
    all_first = jnp.sum(jnp.where(owners[None, :] < mine, by_source, 0), axis=1)
    where_bin = jnp.sum(jnp.where(hit, (all_first + lr0)[None, :] + NM * (slot[:, None] - start[None, :]), 0), axis=1)
    bins_all = bins_all.reshape(NY, NM, NZ, EX).transpose(0, 2, 1, 3).reshape(NS, EX)
    lines = jnp.dot(hit.astype(jnp.float32), bins_all, precision=lax.Precision.HIGHEST)
    got = jnp.sum(jnp.where(where_bin[:, None] == e[None, :], lines, 0.0), axis=1)
    got = jnp.round(got).astype(jnp.int32)
    at_hi = (got[:, None] // 64 == jnp.arange(64)[None, :]).astype(jnp.float32)
    suf = jnp.dot(at_hi, suffix.reshape(64, 64), precision=lax.Precision.HIGHEST)
    suf = jnp.sum(jnp.where(got[:, None] % 64 == jnp.arange(64)[None, :], suf, 0.0), axis=1)
    packed_weights = jnp.where(out_idx >= 0, suf / total, 0.0)
    return hist.astype(jnp.int32), packed_rows, packed_weights


def solution(mesh):
    torus = Mesh(mesh.devices.reshape(NY, NZ, NX, NC), AXES)
    return jax.shard_map(
        body,
        mesh=torus,
        in_specs=(P(AXES), P(), P(AXES, None), P(AXES, None)),
        out_specs=(P(), P(AXES, None), P(AXES)),
        check_vma=False,
    )
```

time: 362 us -> 265 us (0.73)
  blocking collectives: 258 us -> 0 us
  Pallas kernels: 0 us -> 217 us
  local copies, waits for them, and re-layouts: 60.7 us -> 10.3 us
  starting transfers between devices: 28 us -> 0 us
  between operations: 3.41 us -> 15.5 us
  other arithmetic: 10.4 us -> 16.3 us
    psum x1 -> x0, blocking collectives: 223 us -> none  [body(): hist = lax.psum(local_hist, DP_GROUP)]
    pallas_call x0 -> x4, Pallas kernels: none -> 217 us  [the longest x1 167 us: exchange_rows(): pl.pallas_call(functools.partial(main_kernel, caps), out_shape=(jax.Shape...]
    all_to_all x2 -> x0, starting transfers between devices: 28 us -> none  [exchange_both(): tiles = lax.all_to_all(tiles, axis, split_axis=0, concat_axis=0, tiled=True)]
    scatter x4 -> x1, local copies, waits for them, and re-layouts: 28.4 us -> 0.52 us  [body(): row = jnp.zeros((1, 1, 128), jnp.int32).at[0, 0, :NO].set(counts)]
    all_gather x2 -> x0, blocking collectives: 23.3 us -> none  [prefix_by_axis(): pieces = lax.all_gather(so_far, axis)]
    another operation x8 -> x9, local copies, waits for them, and re-layouts: 22.6 us -> 1.21 us  [the longest x2 12.1 us: exchange_both(): tiles = tiles.reshape(-1, *inside)]
    unnamed x2 -> x0, blocking collectives: 12 us -> none
    reduce_sum x2 -> x13, other arithmetic: 1.59 us -> 8.92 us  [the longest x3 6.47 us: layout_of(): flow = lambda d: jnp.sum(jnp.where(delta == d, counts, 0), axis=-1)]
  transfers between devices with their start and end apart: 2 -> 0, of which waited for: 0 -> 0; matrix products, arithmetic and copies ran while one was open for 10% -> 0% of each run, Pallas kernels for 0% -> 0%
where the time goes in v1:
time: 265 us; the launch traced here: 262 us
  Pallas kernels  217 us (82%)
  other arithmetic  16.3 us (6%)
  between operations  15.5 us (6%)
  local copies, waits for them, and re-layouts  10.3 us (4%)
    pallas_call x1, Pallas kernels, exchange_rows(): pl.pallas_call(functools.partial(main_kernel, caps), out_shape=(jax.Shape...  167 us
    pallas_call x1, Pallas kernels, exchange_counts(): pl.pallas_call(counts_kernel, out_shape=jax.ShapeDtypeStruct((PLANE, NZ,...  21.5 us
    pallas_call x1, Pallas kernels, unpack_rows(): pl.pallas_call(unpack_kernel, grid=(RECV // block,), out_shape=jax.ShapeD...  14.2 us
    pallas_call x1, Pallas kernels, pack_rows(): pl.pallas_call(pack_kernel, out_shape=jax.ShapeDtypeStruct((PACKED * 16,...  13.7 us
    reduce_sum x3, other arithmetic, layout_of(): flow = lambda d: jnp.sum(jnp.where(delta == d, counts, 0), axis=-1)  6.47 us

profile of v1, /device:TPU:1, one launch (start us, length us, event | category | flops | bytes accessed | tf_op | source)
XLA Modules:
  0.0 261.6 jit_solution(3300216534197712033)
XLA Ops:
  1.5 0.7 add_select_fusion.13
  2.2 0.7 broadcast_select_fusion
  3.8 0.8 fusion.66
  10.8 0.6 fusion.42.pos_ref
  11.9 21.5 %exchange_counts.1 = s32[32,8,1,128]{3,2,1,0:T(1,128)} custom-call(s32[1,1,128]{2,1,0:T(1,128)} %scatter.4.row_ref), custom_call_target="tpu_custom_call" | custom-call | tf_op jit(solution)/shard_map/exchange_counts/pallas_call | solution.py:91
  33.4 5.4 %select_reduce_fusion.24 = (s32[4,8,8]{1,2,0:T(8,128)S(1)}, s32[4,8,8]{1,2,0:T(8,128)S(1)}, s32[4,8,8]{1,2,0:T(8,128)S(1)}, s32[4,8,8]{1,2,0:T(8,128)S(1)}, s32[...) fusion(s32[4,8,8]{1,2,0:T(8,128)S(1)} %add_select_fusion.6, ...), kind=kLoop, calls=%fused_computation.115 | loop fusion | flops 284672 | bytes 42144 | tf_op jit(solution)/shard_map/reduce_sum | solution.py:310
  38.8 0.9 slice_bitcast_fusion
  39.7 0.8 maximum_reduce_fusion.2
  49.9 0.7 select_reduce_fusion.17
  50.6 0.6 broadcast_add_fusion.1.idx_ref
  52.9 13.7 %pack_rows.1 = s32[14336,128]{1,0:T(8,128)} custom-call(s32[512]{0:T(512)} %fusion.42.pos_ref, s32[8192,128]{1,0:T(8,128)} %bitcast.103), custom_call_target="tpu_custom_call" | custom-call | tf_op jit(solution)/shard_map/pack_rows/pallas_call | solution.py:120
  66.7 173.5 %conditional.2 = (f32[32,128]{1,0:T(8,128)}, (s32[1024,16,128]{2,1,0:T(8,128)}, f32[32,128]{1,0:T(8,128)S(1)}, f32[32,8,4,128]{3,2,1,0:T(4,128)S(1)})) conditional(s32[]{:T(128)} %clamp.3, (s32[8,32]{1,0:T(8,128)S(1)}, s32[32,1]{0,1:T(1,128)S(1)}, s32[1024]{0:T(1024)S(1)}, s32[8,32]{1,0:T(8,128)S(1)}, ...), branch_computations={%region_30.35_spmd.clone, %region_35.40_spmd.clone, %region_40.45_... | conditional | flops 875256 | bytes 1317576
  67.1 0.6 convert_bitcast_fusion.1.bin_ref
  68.9 0.6 gather_fusion.4
  71.5 0.6 fusion.6.idx_ref
  72.1 167.3 %exchange_rows_1.5 = (s32[1024,16,128]{2,1,0:T(8,128)}, f32[32,128]{1,0:T(8,128)}, f32[32,8,4,128]{3,2,1,0:T(4,128)S(1)}) custom-call(s32[1024]{0:T(1024)} %fusion.6.idx_ref, s32[896,16,128]{2,1,0:T(8,128)} %bitcast.98, f32[4,128]{1,0:T(4,128)} %convert_bitcast_fusion.1.bin_ref, f32[32,128]{1,0:T(8,128)S(1)} %get-tuple-element.1665.hist_ref), custom_call_target="tpu_custom_call" | custom-call | tf_op jit(solution)/shard_map/cond/branch_1_fun/exchange_rows_1/pallas_call | solution.py:254
  239.4 0.7 copy.303
  240.7 1.3 select_reduce_fusion.16
  242.0 14.2 %unpack_rows.1 = s32[16384,128]{1,0:T(8,128)} custom-call(s32[1024]{0:T(1024)} %broadcast_add_fusion.1.idx_ref, s32[16384,128]{1,0:T(8,128)} %bitcast.102), custom_call_target="tpu_custom_call" | custom-call | tf_op jit(solution)/shard_map/unpack_rows/pallas_call | solution.py:291
  256.2 0.8 rev.6
  257.7 0.6 dynamic_slice.11
  259.0 0.6 fusion.16
  259.6 0.6 divide_select_fusion
  260.2 1.3 bitcast_convert_fusion
  (90 shorter events, 10.3 us)
